TPU v7x, 128 devices: a whole 4x4x4 slice. The times are simulated.
128 devices in a mesh: tile: 8 (over x, core), tm: 16 (over z, y).
Axes of the slice: x: 4, y: 4, z: 4, core: 2. Of those that a mesh axis runs over, the one named last changes fastest.
Arguments:
- ocean_heat_anomaly: bfloat16 [512, 192, 1024], P('tm', 'tile'), may hold values from -6 to 6
- observation_reliability: bfloat16 [512, 192, 1024], P('tm', 'tile'), may hold values from 0.099609375 to 1
- swath_date_number: int32 [512], replicated, may hold values from 0 to 511, as said below
- marine_cell_flag: int32 [192, 1024], P('tile'), may hold values 0 or 1
Outputs:
- trend: float32 [512, 192, 1024], P('tm', 'tile')
Inputs may be any that keep to these rules, and one draw needn't show every extreme that they name: `swath_date_number`: every day appears exactly once; every index of tm holds the same number of granules of every block of 32 consecutive days, in no particular order.
All inputs are finite; a program needn't handle non-finite values. No bound on the sum of `marine_cell_flag` on one device may be relied on, other than what follows from the above.
Results may differ from a plain program's by a relative error of at most 0.0015.
Values may be sent and summed in bfloat16 or wider, within the bound.
A program may use at most 128 MiB of HBM per device.

v0:
```python
import math

import jax
import jax.numpy as jnp
from jax import lax
from jax.sharding import PartitionSpec as P

DECAY = 0.999
UNIT = 256.0
RIDGE = 0.05


def side_by_side(arrays, axis, dim, along):
    widths = [a.shape[along] for a in arrays]
    both = jnp.concatenate(arrays, axis=along)
    out = lax.all_gather(both, axis, axis=dim, tiled=True)
    return tuple(jnp.split(out, [sum(widths[:k]) for k in range(1, len(widths))], axis=along))


def extended(array, sides, width):
    for axis, dim in sides:
        devices, length = (lax.axis_size(axis), array.shape[dim])
        up = [(i, (i + 1) % devices) for i in range(devices - 1)]
        down = [(j, i) for i, j in up]
        last = lax.slice_in_dim(array, length - width, length, axis=dim)
        leading = lax.slice_in_dim(array, 0, width, axis=dim)
        before = lax.ppermute(last, axis, up)
        after = lax.ppermute(leading, axis, down)
        array = jnp.concatenate([before, array, after], axis=dim)
    return array


def shifted(state, length):
    zeroth, first, second, level_sum, slope_sum = state
    factor = jnp.exp(length * math.log(DECAY))
    offset = length / UNIT
    return (
        factor * zeroth,
        factor * (first + offset * zeroth),
        factor * (second + 2.0 * offset * first + offset * offset * zeroth),
        factor * level_sum,
        factor * (slope_sum + offset * level_sum),
    )


def combine(earlier, later):
    moved = shifted(earlier[:5], later[5])
    joined = tuple((moved[index] + later[index] for index in range(5)))
    return joined + (earlier[5] + later[5],)


def on_device(ocean_heat_anomaly, observation_reliability, swath_date_number, marine_cell_flag):
    ntm = lax.axis_size("tm")
    me_time = lax.axis_index("tm")
    dates_for_shard = ocean_heat_anomaly.shape[0]
    share = dates_for_shard // ntm
    ocean = marine_cell_flag.astype(jnp.float32)
    all_days = swath_date_number.reshape(ntm, dates_for_shard)
    sort_keys = (
        all_days // dates_for_shard * dates_for_shard
        + jnp.arange(dates_for_shard, dtype=jnp.int32)[None]
    )
    send_order = jnp.argsort(sort_keys, axis=1)
    sorted_days = jnp.take_along_axis(all_days, send_order, axis=1)
    shard_ranking_permutation = lax.dynamic_index_in_dim(send_order, me_time, 0, keepdims=False)
    arrived = lax.dynamic_index_in_dim(
        sorted_days.reshape(ntm, ntm, share), me_time, 1, keepdims=False
    )
    positions = arrived.reshape(dates_for_shard) - me_time * dates_for_shard
    lag = jnp.arange(dates_for_shard, dtype=jnp.int32)[:, None] - positions[None, :]
    lag_days = lag.astype(jnp.float32)
    kernel_zero = jnp.where(lag >= 0, jnp.exp(lag_days * math.log(DECAY)), jnp.float32(0.0))
    kernel_one = kernel_zero * (lag_days / UNIT)
    kernel_two = kernel_one * (lag_days / UNIT)
    weight_kernel = jnp.concatenate([kernel_zero, kernel_one, kernel_two], axis=0)
    weight_high = weight_kernel.astype(jnp.bfloat16)
    weight_low = (weight_kernel - weight_high.astype(jnp.float32)).astype(jnp.bfloat16)
    value_kernel = jnp.concatenate([kernel_zero, kernel_one], axis=0)
    ranked_anomaly_field = ocean_heat_anomaly[shard_ranking_permutation]
    sorted_quality = observation_reliability[shard_ranking_permutation]
    anomaly_slice = lax.all_to_all(
        ranked_anomaly_field, "tm", split_axis=0, concat_axis=0, tiled=True
    )
    reliability_slice = lax.all_to_all(
        sorted_quality, "tm", split_axis=0, concat_axis=0, tiled=True
    )
    pointwise_multiple = reliability_slice.astype(jnp.float32) * anomaly_slice.astype(jnp.float32)
    weight_terms = jnp.einsum(
        "ks,src->krc", weight_high, reliability_slice, preferred_element_type=jnp.float32
    ) + jnp.einsum("ks,src->krc", weight_low, reliability_slice, preferred_element_type=jnp.float32)
    value_terms = jnp.einsum(
        "ks,src->krc",
        value_kernel,
        pointwise_multiple,
        precision=lax.Precision.HIGH,
        preferred_element_type=jnp.float32,
    )
    local = (
        weight_terms[:dates_for_shard],
        weight_terms[dates_for_shard : 2 * dates_for_shard],
        weight_terms[2 * dates_for_shard :],
        value_terms[:dates_for_shard],
        value_terms[dates_for_shard:],
    )
    local = tuple((part * ocean[None] for part in local))
    totals = tuple((part[dates_for_shard - 1] for part in local)) + (jnp.float32(dates_for_shard),)
    stacked = side_by_side(
        (totals[0][None], totals[1][None], totals[2][None], totals[3][None], totals[4][None]),
        "tm",
        0,
        1,
    )
    empty = jnp.zeros(ocean.shape, jnp.float32)

    def fold_block(index, state):
        element = tuple(
            (lax.dynamic_index_in_dim(part, index, 0, keepdims=False) for part in stacked)
        )
        merged = combine(state, element + (jnp.float32(dates_for_shard),))
        return tuple((jnp.where(index < me_time, new, old) for new, old in zip(merged, state)))

    carried = lax.fori_loop(
        0, ntm, fold_block, (empty, empty, empty, empty, empty, jnp.float32(0.0))
    )
    offsets = jnp.arange(1, dates_for_shard + 1, dtype=jnp.float32)[:, None, None]
    moved = shifted(tuple((part[None] for part in carried[:5])), offsets)
    zeroth, first, second, level_sum, slope_sum = (
        local[index] + moved[index] for index in range(5)
    )
    det = zeroth * (second + RIDGE) - first * first
    det = jnp.where(ocean[None] > 0, det, jnp.float32(1.0))
    slope = (first * level_sum - zeroth * slope_sum) / det
    stacked_fields = jnp.concatenate([slope, ocean[None]], axis=0)
    padded = extended(stacked_fields, (("tile", 1),), 1)
    padded = jnp.pad(padded, ((0, 0), (0, 0), (1, 1)))
    rowsum = padded[:, :-2] + padded[:, 1:-1] + padded[:, 2:]
    total = rowsum[:, :, :-2] + rowsum[:, :, 1:-1] + rowsum[:, :, 2:]
    count = jnp.maximum(total[dates_for_shard], 1.0)
    return total[:dates_for_shard] / count[None]


def solution(mesh):
    in_specs = (P("tm", "tile", None), P("tm", "tile", None), P(), P("tile", None))
    out_specs = P("tm", "tile", None)
    return jax.shard_map(
        on_device, mesh=mesh, in_specs=in_specs, out_specs=out_specs, check_vma=False
    )
```

profile of v0, /device:TPU:2, one launch (start us, length us, event | category | flops | bytes accessed | tf_op | source)
XLA Modules:
  0.0 225.5 jit_solution(9218020792103862539)
XLA Ops:
  6.5 0.9 reshape.82
  7.5 0.8 sort.17
  8.5 1.8 gather_fusion
  10.3 8.0 %all-to-all-start = ((bf16[32,24,1024]{2,1,0:T(8,128)(2,1)}), bf16[32,24,1024]{2,1,0:T(8,128)(2,1)S(1)}, u32[]{:S(2)}, u32[]{:S(2)}) async-start(bf16[32,24,1024]{2,1,0:T(8,128)(2,1)} %gather_fusion), calls=%async_computation | async-start | bytes 3145728 | tf_op jit(solution)/shard_map/all_to_all | solution.py:84
  18.4 3.2 %gather_fusion.1 = bf16[32,24,1024]{2,1,0:T(8,128)(2,1)} fusion(bf16[32,24,1024]{2,1,0:T(8,128)(2,1)} %param.6, s32[1024]{0:T(1024)S(1)} %pad_clamp_fusion), kind=kCustom, calls=%fused_computation.1 | custom fusion | bytes 3145856 | tf_op jit(solution)/shard_map/gather | solution.py:79
  21.6 21.3 %all-to-all-done = bf16[32,24,1024]{2,1,0:T(8,128)(2,1)S(1)} async-done(((bf16[32,24,1024]{2,1,0:T(8,128)(2,1)}), bf16[32,24,1024]{2,1,0:T(8,128)(2,1)S(1)}, u32[]{:S(2)}, u32[]{:S(2)}) %all-to-all-start) | async-done | bytes 1572896 | tf_op jit(solution)/shard_map/all_to_all | solution.py:84
  42.9 4.4 %all-to-all-start.1 = ((bf16[32,24,1024]{2,1,0:T(8,128)(2,1)}), bf16[32,24,1024]{2,1,0:T(8,128)(2,1)}, u32[]{:S(2)}, u32[]{:S(2)}) async-start(bf16[32,24,1024]{2,1,0:T(8,128)(2,1)} %gather_fusion.1), calls=%async_computation.1 | async-start | bytes 3145728 | tf_op jit(solution)/shard_map/all_to_all | solution.py:81
  47.5 3.8 %gather_fusion.2 = s32[512]{0:T(512)S(1)} fusion(s32[16,32]{1,0:T(8,128)S(1)} %reshape.82, s32[512]{0:T(512)S(1)} %reshape.100), kind=kCustom, calls=%fused_computation.2 | custom fusion | bytes 8192 | tf_op jit(solution)/shard_map/jit(take_along_axis)/gather | solution.py:64
  51.8 17.7 %all-to-all-done.1 = bf16[32,24,1024]{2,1,0:T(8,128)(2,1)} async-done(((bf16[32,24,1024]{2,1,0:T(8,128)(2,1)}), bf16[32,24,1024]{2,1,0:T(8,128)(2,1)}, u32[]{:S(2)}, u32[]{:S(2)}) %all-to-all-start.1) | async-done | bytes 1572896 | tf_op jit(solution)/shard_map/all_to_all | solution.py:81
  69.5 2.0 convert_multiply_fusion
  71.5 4.4 %fusion.6 = f32[64,24,1024]{2,0,1:T(8,128)S(1)} fusion(f32[32,24,1024]{2,1,0:T(8,128)S(1)} %convert_multiply_fusion, f32[32,32]{0,1:T(8,128)S(1)} %get-tuple-element.337, f32[32,32]{0,1:T(8,128)S(1)} %get-tuple-element.336), kind=kOutput, calls=%fused_computation.30 | convolution fusion | flops 301991936 | bytes 9445376 | tf_op jit(solution)/shard_map/ks,src->krc/dot_general | solution.py:91
  76.0 2.5 %fusion.9 = f32[96,24,1024]{2,0,1:T(8,128)S(1)} fusion(bf16[32,24,1024]{2,1,0:T(8,128)(2,1)S(1)} %all-to-all-done, f32[32,32]{0,1:T(8,128)S(1)} %get-tuple-element.338, f32[32,32]{0,1:T(8,128)S(1)} %get-tuple-element.337, f32[32,32]{0,1:T(8,128)S(1)} %get-tuple-element.336), kind=kOutput, calls=%fused_computation.35 | convolution fusion | flops 151013376 | bytes 11022336 | tf_op jit(solution)/shard_map/ks,src->krc/dot_general | solution.py:88
  78.5 3.0 %convolution_add_fusion = f32[96,24,1024]{2,0,1:T(8,128)S(1)} fusion(f32[96,24,1024]{2,0,1:T(8,128)S(1)} %fusion.9, bf16[32,24,1024]{2,1,0:T(8,128)(2,1)S(1)} %all-to-all-done, f32[32,32]{0,1:T(8,128)S(1)} %get-tuple-element.338, f32[32,32]{0,1:T(8,128)S(1)} %get-tuple-element.337, f32[32,32]{0,1:T(8,128)S(1)} %get-tuple-element.336), kind=kOutput, calls=%fused_computation.23 | convolution fusion | flops 153372672 | bytes 20459520 | tf_op jit(solution)/shard_map/ks,src->krc/dot_general | solution.py:90
  81.6 4.4 %slice_multiply_fusion.4 = (f32[32,24,1024]{2,0,1:T(8,128)S(1)}, f32[32,24,1024]{2,0,1:T(8,128)S(1)}, f32[32,24,1024]{2,0,1:T(8,128)}, f32[32,24,1024]{2,0,1:T(8,128)}, f32[32,24,1024]{2,0,1:T(8,128)}) fusion(f32[96,24,1024]{2,0,1:T(8,128)S(1)} %convolution_add_fusion, f32[24,1024]{1,0:T(8,128)S(1)} %convert_element_type.27, f32[64,24,1024]{2,0,1:T(8,128)S(1)} %fusion.6), kind=kLoop, calls=%fused_computation.29 | loop fusion | flops 3932160 | bytes 31555584 | tf_op jit(solution)/shard_map/mul | solution.py:105
  86.0 1.8 slice_dynamic-update-slice_fusion.4
  88.0 1.2 slice_dynamic-update-slice_fusion.1
  89.2 1.2 slice_dynamic-update-slice_fusion
  90.5 0.9 copy.49
  91.4 1.6 broadcast_in_dim.25
  93.0 1.5 broadcast_compare_fusion
  94.5 62.9 %all-gather.2.cloned.1.call-done = f32[16,120,1024]{2,1,0:T(8,128)} async-done(((f32[1,120,1024]{2,1,0:T(8,128)}), f32[16,120,1024]{2,1,0:T(8,128)}) %all-gather.2.cloned.1.call-update) | async-done | bytes 7864336 | tf_op jit(solution)/shard_map/all_gather | solution.py:16
  157.4 6.6 %fusion.30 = (f32[16,24,1024]{2,1,0:T(8,128)}, f32[16,24,1024]{2,1,0:T(8,128)}, f32[16,24,1024]{2,1,0:T(8,128)}, f32[16,24,1024]{2,1,0:T(8,128)}, f32[16,24,1024]{2,1,0:T(8,128)}) fusion(f32[16,120,1024]{2,1,0:T(8,128)} %all-gather.2.cloned.1.call-done), kind=kLoop, calls=%fused_computation.85 | loop fusion | bytes 15728640 | tf_op jit(solution)/shard_map/split | solution.py:17
  164.0 29.8 %while.22 = (s32[]{:T(128)}, f32[24,1024]{1,0:T(8,128)S(1)}, f32[24,1024]{1,0:T(8,128)S(1)}, f32[24,1024]{1,0:T(8,128)S(1)}, f32[24,1024]{1,0:T(8,128)S(1)}, /*i...) while((s32[]{:T(128)}, f32[24,1024]{1,0:T(8,128)S(1)}, ...), condition=%wide.region_2.3_spmd.clone, body=%wide.region_1.2_spmd.clone.sunk | while | flops 688132 | bytes 1474717 | solution.py:122
  164.0 1.8 fusion.32
  165.9 1.9 fusion.32
  167.7 1.9 fusion.32
  169.6 1.9 fusion.32
  171.5 1.9 fusion.32
  173.3 1.9 fusion.32
  175.2 1.9 fusion.32
  177.0 1.9 fusion.32
  178.9 1.9 fusion.32
  180.8 1.9 fusion.32
  182.6 1.9 fusion.32
  184.5 1.9 fusion.32
  186.4 1.9 fusion.32
  188.2 1.9 fusion.32
  190.1 1.9 fusion.32
  192.0 1.9 fusion.32
  193.8 6.6 %select_divide_fusion = f32[32,24,1024]{2,0,1:T(8,128)S(1)} fusion(f32[32,24,1024]{2,0,1:T(8,128)} %copy-done.2, f32[32,24,1024]{2,0,1:T(8,128)} %get-tuple-element.334, f32[32,24,1024]{2,0,1:T(8,128)} %get-tuple-element.324, f32[32,24,1024]{2,0,1:T(8,128)} %get-tuple-element.335, f32[32,24,1024]{2,0,1:T(8,128)S(1)} %get-tuple-element.322, ...), kind=kLoop, calls=%fused_computation.32 | loop fusion | flops 21233664 | bytes 19390976 | tf_op jit(solution)/shard_map/div | solution.py:132
  200.4 1.9 collective-permute-start
  202.4 3.6 %collective-permute-start.1 = (f32[33,1,1024]{2,0,1:T(8,128)S(1)}, f32[33,1,1024]{2,0,1:T(8,128)S(1)}, u32[]{:S(2)}, u32[]{:S(2)}) collective-permute-start(f32[33,1,1024]{2,0,1:T(8,128)S(1)} %get-tuple-element.333), channel_id=1, source_target_pairs={{16,0},{32,16},{48,32},{64,48},{80,64},{96,80},{112,96},{17,1},{33... | collective-permute-start | bytes 405512 | tf_op jit(solution)/shard_map/ppermute | solution.py:28
  206.0 1.1 collective-permute-done
  207.1 1.8 collective-permute-done.1
  208.8 3.3 %select_maximum_fusion = f32[33,26,1026]{2,0,1:T(8,128)S(1)} fusion(f32[33,1,1024]{2,0,1:T(8,128)S(1)} %collective-permute-done.1, f32[33,1,1024]{2,0,1:T(8,128)S(1)} %collective-permute-done, f32[1,24,1024]{2,0,1:T(1,128)S(1)} %copy-done.3, f32[32,24,1024]{2,0,1:T(8,128)S(1)} %select_divide_fusion), kind=kLoop, calls=%fused_computation.15 | loop fusion | flops 8803080 | bytes 7035600 | tf_op jit(solution)/shard_map/concatenate | solution.py:29
  212.5 2.1 slice_add_fusion.2
  214.7 0.4 slice_divide_fusion
  215.1 3.5 %copy.50 = f32[32,24,1024]{2,1,0:T(8,128)} copy(f32[32,24,1024]{2,0,1:T(8,128)S(1)} %slice_divide_fusion) | data formatting | bytes 6291456 | tf_op jit(solution)/shard_map/div | solution.py:139
  (44 shorter events, 1.6 us)
Async XLA Ops:
  6.5 2.0 copy-start
  10.3 32.6 %all-to-all-start = ((bf16[32,24,1024]{2,1,0:T(8,128)(2,1)}), bf16[32,24,1024]{2,1,0:T(8,128)(2,1)S(1)}, u32[]{:S(2)}, u32[]{:S(2)}) async-start(bf16[32,24,1024]{2,1,0:T(8,128)(2,1)} %gather_fusion), calls=%async_computation | async-start | bytes 3145728 | tf_op jit(solution)/shard_map/all_to_all | solution.py:84
  42.9 26.6 %all-to-all-start.1 = ((bf16[32,24,1024]{2,1,0:T(8,128)(2,1)}), bf16[32,24,1024]{2,1,0:T(8,128)(2,1)}, u32[]{:S(2)}, u32[]{:S(2)}) async-start(bf16[32,24,1024]{2,1,0:T(8,128)(2,1)} %gather_fusion.1), calls=%async_computation.1 | async-start | bytes 3145728 | tf_op jit(solution)/shard_map/all_to_all | solution.py:81
  47.3 110.1 %all-gather.2.cloned.1.call-start = ((), (), s32[]{:S(2)}) async-start(), calls=%async_computation.2 | async-start | bytes 8355840 | tf_op jit(solution)/shard_map/all_gather | solution.py:16
  47.5 4.1 %copy-start.5 = (s32[24,1024]{1,0:T(8,128)S(1)}, s32[24,1024]{1,0:T(8,128)}, u32[]{:S(2)}) copy-start(s32[24,1024]{1,0:T(8,128)} %param.9) | copy-start | bytes 294916
  51.7 29.9 %copy-start.4 = (f32[24,1024]{1,0:T(8,128)}, f32[24,1024]{1,0:T(8,128)S(1)}, u32[]{:S(2)}) copy-start(f32[24,1024]{1,0:T(8,128)S(1)} %convert_element_type.27) | copy-start | bytes 294916
  86.0 1.9 copy-start.2
  193.8 6.6 %copy-start.3 = (f32[1,24,1024]{2,0,1:T(1,128)S(1)}, f32[1,24,1024]{2,0,1:T(1,128)}, u32[]{:S(2)}) copy-start(f32[1,24,1024]{2,0,1:T(1,128)} %broadcast_in_dim.25) | copy-start | bytes 294916
  200.4 6.6 %collective-permute-start = (f32[33,1,1024]{2,0,1:T(8,128)S(1)}, f32[33,1,1024]{2,0,1:T(8,128)S(1)}, u32[]{:S(2)}, u32[]{:S(2)}) collective-permute-start(f32[33,1,1024]{2,0,1:T(8,128)S(1)} %get-tuple-element.332), channel_id=1, source_target_pairs={{0,16},{16,32},{32,48},{48,64},{64,80},{80,96},{96,112},{1,17},{17... | collective-permute-start | bytes 405512 | tf_op jit(solution)/shard_map/ppermute | solution.py:27
  202.4 6.5 %collective-permute-start.1 = (f32[33,1,1024]{2,0,1:T(8,128)S(1)}, f32[33,1,1024]{2,0,1:T(8,128)S(1)}, u32[]{:S(2)}, u32[]{:S(2)}) collective-permute-start(f32[33,1,1024]{2,0,1:T(8,128)S(1)} %get-tuple-element.333), channel_id=1, source_target_pairs={{16,0},{32,16},{48,32},{64,48},{80,64},{96,80},{112,96},{17,1},{33... | collective-permute-start | bytes 405512 | tf_op jit(solution)/shard_map/ppermute | solution.py:28
  214.7 3.9 %copy-start.1 = (bf16[32,24,1024]{2,1,0:T(8,128)(2,1)S(1)}, bf16[32,24,1024]{2,1,0:T(8,128)(2,1)}, u32[]{:S(2)}) copy-start(bf16[32,24,1024]{2,1,0:T(8,128)(2,1)} %param.7) | copy-start | bytes 4718596
Sparse Core Ops, SparseCore 0:
  91.5 65.9 all-gather.1
where the time goes:
time: 229 us; the launch traced here: 225 us
  waiting for transfers between devices  105 us (46%)
  other arithmetic  51.5 us (22%)
  local copies, waits for them, and re-layouts  27.4 us (12%)
  starting transfers between devices  18.1 us (8%)
  between operations  13.7 us (6%)
  matrix products  10 us (4%)
    all_gather x1, waiting for transfers between devices, side_by_side(): out = lax.all_gather(both, axis, axis=dim, tiled=True)  62.9 us
    select_n x16, other arithmetic, fold_block(): jnp.where(index < me_time, new, old)  29.8 us
    all_to_all x1, waiting for transfers between devices, on_device(): lax.all_to_all(sorted_quality, 'tm', split_axis=0, concat_axis=0, tiled=T...  21.3 us
    all_to_all x1, waiting for transfers between devices, on_device(): lax.all_to_all(ranked_anomaly_field, 'tm', split_axis=0, concat_axis=0, t...  17.7 us
    all_to_all x1, starting transfers between devices, on_device(): lax.all_to_all(sorted_quality, 'tm', split_axis=0, concat_axis=0, tiled=T...  8.05 us
    split x1, local copies, waits for them, and re-layouts, side_by_side(): jnp.split(out, [sum(widths[:k]) for k in range(1, len(widths))], axis=along)  6.58 us
    div x1, other arithmetic, on_device(): slope = (first * level_sum - zeroth * slope_sum) / det  6.55 us
  transfers between devices with their start and end apart: 5, of which 5 were waited for; matrix products, arithmetic and copies ran while one was open for 5% of the time, Pallas kernels for 0%

commit v1 on v0

v1 whole, which is shorter than its diff:
```python
import functools
import math

import jax
import jax.numpy as jnp
from jax import lax
from jax.experimental import pallas as pl
from jax.experimental.pallas import tpu as pltpu
from jax.sharding import PartitionSpec as P

DECAY = 0.999
UNIT = 256.0
RIDGE = 0.05
MESH = pl.DeviceIdType.MESH

OFFSETS = (
    (0, 1), (1, 0), (0, 3), (3, 0), (1, 1), (3, 3), (1, 3), (3, 1),
    (2, 0), (0, 2), (2, 1), (1, 2), (2, 3), (3, 2), (2, 2),
)
CHUNKS = (0, 2, 1)
GROUP = 2


def wait_bytes(ref, sem):
    pltpu.make_async_copy(ref, ref, sem).wait()


def exchange_kernel(
    days, ints_ref, floats_ref, x_ref, w_ref, mask_ref,
    slope_ref, halo_ref, mhalo_ref,
    stage, recv, tsend, trecv, csend, crecv, edge, hrecv, mrecv,
    g_send, g_recv, t_send, t_recv, c_send, c_recv, h_send, h_recv, m_send, m_recv,
):
    me = lax.axis_index("tm")
    tile = lax.axis_index("tile")
    z, y = me // 4, lax.rem(me, 4)
    peers = [lax.rem(z + dz, 4) * 4 + lax.rem(y + dy, 4) for dz, dy in OFFSETS]
    above, below = lax.rem(tile + 7, 8), lax.rem(tile + 1, 8)
    nchunk = len(CHUNKS)

    barrier = pltpu.get_barrier_semaphore()
    for p in peers:
        pl.semaphore_signal(barrier, inc=1, device_id={"tm": p}, device_id_type=MESH)
    for t in (above, below):
        pl.semaphore_signal(barrier, inc=1, device_id={"tile": t}, device_id_type=MESH)

    def place(k, _):
        i = ints_ref[k]
        for c in range(nchunk):
            stage[c, k, 0] = x_ref[i, 4 * c : 4 * c + 4]
            stage[c, k, 1] = w_ref[i, 4 * c : 4 * c + 4]
        return _

    lax.fori_loop(0, days, place, 0)
    for j in range(2):
        i = ints_ref[2 * me + j]
        for c in range(nchunk):
            recv[c, 2 * me + j, 0] = x_ref[i, 4 * c : 4 * c + 4]
            recv[c, 2 * me + j, 1] = w_ref[i, 4 * c : 4 * c + 4]
    pl.semaphore_wait(barrier, len(peers) + 2)

    def remote(src, dst, send, arrive, where):
        pltpu.make_async_remote_copy(
            src_ref=src, dst_ref=dst, send_sem=send, recv_sem=arrive,
            device_id=where, device_id_type=MESH,
        ).start()

    def send_granules(c):
        for p in peers:
            remote(
                stage.at[c, pl.ds(2 * p, 2)], recv.at[c, pl.ds(2 * me, 2)],
                g_send.at[c], g_recv.at[c], {"tm": p},
            )

    def block_totals(c):
        wait_bytes(recv.at[c, pl.ds(0, 30)], g_recv.at[c])
        for g in range(4 // GROUP):
            def add(s, state):
                zeroth, first, second, level, slope = state
                a, u = floats_ref[s], floats_ref[days + s]
                v = recv[c, s, 0, GROUP * g : GROUP * (g + 1)].astype(jnp.float32)
                w = recv[c, s, 1, GROUP * g : GROUP * (g + 1)].astype(jnp.float32) * a
                wu = w * u
                p = w * v
                return (zeroth + w, first + wu, second + wu * u, level + p, slope + p * u)

            empty = jnp.zeros((GROUP, 16, 128), jnp.float32)
            state = lax.fori_loop(0, days, add, (empty,) * 5)
            for m in range(5):
                for q in range(GROUP):
                    for k in range(4):
                        tsend[c, 4 * (GROUP * g + q) + k, m] = state[m][q, 4 * k : 4 * k + 4, :]
        trecv[c, me] = tsend[c, me]
        for p in peers:
            remote(tsend.at[c, p], trecv.at[c, me], t_send.at[c], t_recv.at[c], {"tm": p})

    factor, offset = DECAY**days, days / UNIT

    def carries(c):
        wait_bytes(trecv.at[c, pl.ds(0, 15)], t_recv.at[c])
        state = [jnp.zeros((4, 128), jnp.float32)] * 5
        for b in range(16):
            zeroth, first, second, level, slope = state
            moved = (
                factor * zeroth,
                factor * (first + offset * zeroth),
                factor * (second + (2 * offset) * first + (offset * offset) * zeroth),
                factor * level,
                factor * (slope + offset * level),
            )
            for m in range(5):
                csend[c, b, m] = moved[m]
            state = [moved[m] + trecv[c, b, m] for m in range(5)]
        crecv[c, me] = csend[c, me]
        for p in peers:
            remote(csend.at[c, p], crecv.at[c, me], c_send.at[c], c_recv.at[c], {"tm": p})

    def slopes(c):
        wait_bytes(crecv.at[c, pl.ds(0, 15)], c_recv.at[c])
        for g in range(4 // GROUP):
            start = tuple(
                jnp.stack([
                    jnp.concatenate([crecv[c, 4 * (GROUP * g + q) + k, m] for k in range(4)], axis=0)
                    for q in range(GROUP)
                ])
                for m in range(5)
            )

            def advance(d, state):
                zeroth, first, second, level, slope = state
                s = ints_ref[days + d]
                a, u, ridge = (floats_ref[(2 + n) * days + d] for n in range(3))
                v = recv[c, s, 0, GROUP * g : GROUP * (g + 1)].astype(jnp.float32)
                w = recv[c, s, 1, GROUP * g : GROUP * (g + 1)].astype(jnp.float32) * a
                wu = w * u
                p = w * v
                zeroth, first, second = zeroth + w, first + wu, second + wu * u
                level, slope = level + p, slope + p * u
                det = zeroth * (second + ridge) - first * first
                out = (first * level - zeroth * slope) / det
                for q in range(GROUP):
                    for h in range(2):
                        lanes = pl.ds(128 * (2 * (GROUP * g + q) + h), 128)
                        value = out[q, 8 * h : 8 * h + 8, :]
                        value = jnp.where(mask_ref[8 * c : 8 * c + 8, lanes] > 0, value, 0.0)
                        slope_ref[d, 8 * c : 8 * c + 8, lanes] = value
                        if c == 0:
                            edge[0, d, 2 * (GROUP * g + q) + h : 2 * (GROUP * g + q) + h + 1] = value[0:1]
                        if c == nchunk - 1:
                            edge[1, d, 2 * (GROUP * g + q) + h : 2 * (GROUP * g + q) + h + 1] = value[7:8]
                return (zeroth, first, second, level, slope)

            lax.fori_loop(0, days, advance, start)
        if c == 0:
            remote(edge.at[0], hrecv.at[1], h_send.at[0], h_recv.at[1], {"tile": above})
        if c == nchunk - 1:
            remote(edge.at[1], hrecv.at[0], h_send.at[1], h_recv.at[0], {"tile": below})

    remote(mask_ref.at[0:8], mrecv.at[1], m_send.at[0], m_recv.at[1], {"tile": above})
    remote(mask_ref.at[16:24], mrecv.at[0], m_send.at[1], m_recv.at[0], {"tile": below})

    first, middle, last = CHUNKS
    send_granules(first)
    send_granules(middle)
    block_totals(first)
    send_granules(last)
    block_totals(middle)
    carries(first)
    block_totals(last)
    carries(middle)
    slopes(first)
    carries(last)
    slopes(middle)
    slopes(last)

    for n in range(2):
        wait_bytes(mrecv.at[n], m_recv.at[n])
        wait_bytes(hrecv.at[n], h_recv.at[n])
    halo_ref[...] = hrecv[...]
    mhalo_ref[...] = mrecv[...]
    for c in range(nchunk):
        wait_bytes(stage.at[c, pl.ds(0, 30)], g_send.at[c])
        wait_bytes(tsend.at[c, pl.ds(0, 15)], t_send.at[c])
        wait_bytes(csend.at[c, pl.ds(0, 15)], c_send.at[c])
    for n in range(2):
        wait_bytes(edge.at[n], h_send.at[n])
        wait_bytes(mask_ref.at[0:8], m_send.at[n])


def box_sum(field, up, down):
    column = lax.broadcasted_iota(jnp.int32, field.shape, 1)
    rows = (
        field
        + jnp.concatenate([up, field[:-1]], axis=0)
        + jnp.concatenate([field[1:], down], axis=0)
    )
    width = field.shape[1]
    left = jnp.where(column == 0, 0.0, pltpu.roll(rows, 1, 1))
    right = jnp.where(column == width - 1, 0.0, pltpu.roll(rows, width - 1, 1))
    return rows + left + right


def row_of(pieces):
    return jnp.concatenate([pieces[k : k + 1] for k in range(pieces.shape[0])], axis=1)


def smooth_kernel(valid_ref, slope_ref, halo_ref, mask_ref, mhalo_ref, out_ref, inverse):
    step, per = pl.program_id(0), slope_ref.shape[0]
    has_up, has_down = valid_ref[0], valid_ref[1]

    @pl.when(step == 0)
    def _():
        count = box_sum(
            mask_ref[...].astype(jnp.float32),
            mhalo_ref[0, 7:8].astype(jnp.float32) * has_up,
            mhalo_ref[1, 0:1].astype(jnp.float32) * has_down,
        )
        inverse[...] = 1.0 / jnp.maximum(count, 1.0)

    for n in range(per):
        d = step * per + n
        up = row_of(halo_ref[0, d]) * has_up
        down = row_of(halo_ref[1, d]) * has_down
        out_ref[n] = box_sum(slope_ref[n], up, down) * inverse[...]


def tables(swath_date_number, me, n, days):
    index = jnp.arange(days, dtype=jnp.int32)
    all_days = swath_date_number.reshape(n, days)
    block = all_days // days
    mine = lax.dynamic_index_in_dim(block, me, 0, keepdims=False)
    key = mine * days + index
    rank = jnp.sum((key[None, :] < key[:, None]).astype(jnp.int32), axis=1)
    order = jnp.sum(jnp.where(rank[None, :] == index[:, None], index[None, :], 0), axis=1)
    inside = block == me
    before = (index[None, :] < index[:, None])[None] & inside[:, None, :]
    place = jnp.sum(before.astype(jnp.int32), axis=2)
    slot = 2 * jnp.arange(n, dtype=jnp.int32)[:, None] + place
    hit = (all_days - me * days)[None] == index[:, None, None]
    slot_of_day = jnp.sum(jnp.where(hit, slot[None], 0), axis=(1, 2))
    day_of_slot = jnp.sum(jnp.where(slot_of_day[None, :] == index[:, None], index[None, :], 0), axis=1)
    ints = jnp.concatenate([order, slot_of_day])
    lag_slot = (days - 1 - day_of_slot).astype(jnp.float32)
    lag_day = (days - 1 - index).astype(jnp.float32)
    decay_slot = jnp.exp(lag_slot * math.log(DECAY))
    decay_day = jnp.exp(lag_day * math.log(DECAY))
    floats = jnp.concatenate(
        [decay_slot, lag_slot / UNIT, decay_day, lag_day / UNIT, RIDGE * decay_day]
    )
    return ints, floats


def tiled(array):
    days, rows, width = array.shape
    parts = array.reshape(days, rows // 8, 8, width // 256, 2, 128)
    return parts.transpose(0, 1, 3, 4, 2, 5).reshape(days, rows // 8 * (width // 256), 16, 128)


def on_device(ocean_heat_anomaly, observation_reliability, swath_date_number, marine_cell_flag):
    n, me, tile = lax.axis_size("tm"), lax.axis_index("tm"), lax.axis_index("tile")
    days, rows, width = ocean_heat_anomaly.shape
    ints, floats = tables(swath_date_number, me, n, days)
    f32, bf16 = jnp.float32, jnp.bfloat16
    smem = pl.BlockSpec(memory_space=pltpu.SMEM)
    vmem = pl.BlockSpec(memory_space=pltpu.VMEM)
    sem = pltpu.SemaphoreType.DMA
    slope, halo, mhalo = pl.pallas_call(
        functools.partial(exchange_kernel, days),
        out_shape=(
            jax.ShapeDtypeStruct((days, rows, width), f32),
            jax.ShapeDtypeStruct((2, days, width // 128, 128), f32),
            jax.ShapeDtypeStruct((2, 8, width), jnp.int32),
        ),
        in_specs=[smem, smem, vmem, vmem, vmem],
        out_specs=(vmem, vmem, vmem),
        scratch_shapes=[
            pltpu.VMEM((3, days, 2, 4, 16, 128), bf16),
            pltpu.VMEM((3, days, 2, 4, 16, 128), bf16),
            pltpu.VMEM((3, n, 5, 4, 128), f32),
            pltpu.VMEM((3, n, 5, 4, 128), f32),
            pltpu.VMEM((3, n, 5, 4, 128), f32),
            pltpu.VMEM((3, n, 5, 4, 128), f32),
            pltpu.VMEM((2, days, width // 128, 128), f32),
            pltpu.VMEM((2, days, width // 128, 128), f32),
            pltpu.VMEM((2, 8, width), jnp.int32),
        ] + [sem((3,))] * 6 + [sem((2,))] * 4,
        compiler_params=pltpu.CompilerParams(collective_id=0, has_side_effects=True),
    )(ints, floats, tiled(ocean_heat_anomaly), tiled(observation_reliability), marine_cell_flag)
    valid = jnp.stack([tile > 0, tile < lax.axis_size("tile") - 1]).astype(f32)
    per = 4
    whole = lambda *shape: pl.BlockSpec(shape, lambda i: (0,) * len(shape))
    return pl.pallas_call(
        smooth_kernel,
        grid=(days // per,),
        out_shape=jax.ShapeDtypeStruct((days, rows, width), f32),
        in_specs=[
            smem,
            pl.BlockSpec((per, rows, width), lambda i: (i, 0, 0)),
            whole(2, days, width // 128, 128),
            whole(rows, width),
            whole(2, 8, width),
        ],
        out_specs=pl.BlockSpec((per, rows, width), lambda i: (i, 0, 0)),
        scratch_shapes=[pltpu.VMEM((rows, width), f32)],
    )(valid, slope, halo, marine_cell_flag, mhalo)


def solution(mesh):
    in_specs = (P("tm", "tile", None), P("tm", "tile", None), P(), P("tile", None))
    out_specs = P("tm", "tile", None)
    return jax.shard_map(
        on_device, mesh=mesh, in_specs=in_specs, out_specs=out_specs, check_vma=False
    )
```

time: 229 us -> 76.1 us (0.33); the launches traced: 225 us -> 75.8 us
  waiting for transfers between devices: 105 us -> 0 us
  Pallas kernels: 0 us -> 71.5 us
  other arithmetic: 51.5 us -> 2.86 us
  local copies, waits for them, and re-layouts: 27.4 us -> 1.42 us
  starting transfers between devices: 18.1 us -> 0 us
  between operations: 13.7 us -> 0.04 us
  matrix products: 10 us -> 0 us
    pallas_call x0 -> x2, Pallas kernels: none -> 71.5 us  [the longest x1 64.2 us: on_device(): pl.pallas_call(functools.partial(exchange_kernel, days), out_shape=(jax.S...]
    all_gather x1 -> x0, waiting for transfers between devices: 62.9 us -> none  [side_by_side(): out = lax.all_gather(both, axis, axis=dim, tiled=True)]
    all_to_all x2 -> x0, waiting for transfers between devices: 39.1 us -> none  [the longest x1 21.3 us: on_device(): lax.all_to_all(sorted_quality, 'tm', split_axis=0, concat_axis=0, tiled=T...]
    select_n x19 -> x0, other arithmetic: 29.9 us -> none  [the longest x16 29.8 us: fold_block(): jnp.where(index < me_time, new, old)]
    all_to_all x2 -> x0, starting transfers between devices: 12.4 us -> none  [the longest x1 8.05 us: on_device(): lax.all_to_all(sorted_quality, 'tm', split_axis=0, concat_axis=0, tiled=T...]
    dot_general x3 -> x0, matrix products: 10 us -> none  [the longest x1 4.43 us: on_device(): jnp.einsum('ks,src->krc', value_kernel, pointwise_multiple, precision=lax...]
    gather x5 -> x0, local copies, waits for them, and re-layouts: 8.91 us -> none  [the longest x3 3.91 us: on_device(): sorted_days = jnp.take_along_axis(all_days, send_order, axis=1)]
    div x3 -> x1, other arithmetic: 6.95 us -> 0.01 us  [tables(): lag_slot / UNIT]
  transfers between devices with their start and end apart: 5 -> 0, of which waited for: 5 -> 0; matrix products, arithmetic and copies ran while one was open for 5% -> 0% of each run, Pallas kernels for 0% -> 0%
where the time goes in v1:
time: 76.1 us; the launch traced here: 75.8 us
  Pallas kernels  71.5 us (94%)
  other arithmetic  2.86 us (4%)
  local copies, waits for them, and re-layouts  1.42 us (2%)
    pallas_call x1, Pallas kernels, on_device(): pl.pallas_call(functools.partial(exchange_kernel, days), out_shape=(jax.S...  64.2 us
    pallas_call x1, Pallas kernels, on_device(): pl.pallas_call(smooth_kernel, grid=(days // per,), out_shape=jax.ShapeDty...  7.29 us

profile of v1, /device:TPU:2, one launch (start us, length us, event | category | flops | bytes accessed | tf_op | source)
XLA Modules:
  0.0 75.8 jit_solution(1458225017826185789)
XLA Ops:
  0.0 0.6 add_convert_fusion.valid_ref
  0.6 0.8 %reshape.95 = s32[16,32]{1,0:T(8,128)S(1)} reshape(s32[512]{0:T(512)} %param.6) | data formatting | bytes 4096 | tf_op jit(solution)/shard_map/reshape | solution.py:229
  1.4 0.2 convert_reduce_fusion.1
  1.6 0.1 select_reduce_fusion.2
  1.7 0.4 convert_reduce_fusion
  2.1 0.1 broadcast_add_fusion
  2.2 0.7 select_reduce_fusion
  2.9 0.7 pad_add_fusion.ints_ref
  3.5 0.1 select_reduce_fusion.1
  3.7 0.7 concatenate.7.floats_ref
  4.3 64.2 %shard_map.46 = (f32[32,24,1024]{2,1,0:T(8,128)}, f32[2,32,8,128]{3,2,1,0:T(8,128)}, s32[2,8,1024]{2,1,0:T(8,128)}) custom-call(s32[64]{0:T(128)} %pad_add_fusion.ints_ref, f32[160]{0:T(256)} %concatenate.7.floats_ref, bf16[32,12,16,128]{3,2,1,0:T(8,128)(2,1)} %bitcast.16, bf16[32,12,16,128]{3,2,1,0:T(8,128)(2,1)} %bitcast.17, s32[24,1024]{1,0:T(8,128)} %mask_ref.3), custom_call_target="tpu_custom_call" | custom-call | tf_op jit(solution)/shard_map/pallas_call | solution.py:267
  68.5 7.3 %shard_map.47 = f32[32,24,1024]{2,1,0:T(8,128)} custom-call(f32[2]{0:T(128)} %add_convert_fusion.valid_ref, f32[32,24,1024]{2,1,0:T(8,128)} %get-tuple-element.8.slope_ref, f32[2,32,8,128]{3,2,1,0:T(8,128)} %get-tuple-element.9.halo_ref, s32[24,1024]{1,0:T(8,128)} %mask_ref.3, s32[2,8,1024]{2,1,0:T(8,128)} %get-tuple-element.10.mhalo_ref), custom_call_target="tpu_custom_call" | custom-call | tf_op jit(solution)/shard_map/pallas_call | solution.py:292
  (8 shorter events, 0.1 us)

commit v2 on v1

v2 whole, which is shorter than its diff:
```python
import functools
import math

import jax
import jax.numpy as jnp
from jax import lax
from jax.experimental import pallas as pl
from jax.experimental.pallas import tpu as pltpu
from jax.sharding import PartitionSpec as P

DECAY = 0.999
UNIT = 256.0
RIDGE = 0.05
MESH = pl.DeviceIdType.MESH

OFFSETS = (
    (0, 1), (1, 0), (0, 3), (3, 0), (1, 1), (3, 3), (1, 3), (3, 1),
    (2, 0), (0, 2), (2, 1), (1, 2), (2, 3), (3, 2), (2, 2),
)
CHUNKS = (0, 2, 1)
GROUP = 2


def wait_bytes(ref, sem):
    pltpu.make_async_copy(ref, ref, sem).wait()


def write_tables(days, me, swath_ref, ints_vec, floats_vec):
    swath = swath_ref[...]
    row, lane = (lax.broadcasted_iota(jnp.int32, swath.shape, k) for k in range(2))
    per = 128 // days
    block, group, index = swath // days, lane // days, lax.rem(lane, days)
    source = per * row + group

    owned = jnp.sum(jnp.where(source == me, block, 0), axis=0, keepdims=True)
    number, lane16 = (lax.broadcasted_iota(jnp.int32, (16, 128), k) for k in range(2))
    index16 = lax.rem(lane16, days)
    match = (number == owned) & (lane16 // days == lax.rem(me, per))
    early = jnp.min(jnp.where(match, index16, days - 1), axis=1, keepdims=True)
    late = jnp.max(jnp.where(match, index16, 0), axis=1, keepdims=True)
    diagonal = number == lane16
    ints_vec[0:1] = jnp.sum(jnp.where(diagonal, early, 0), axis=0, keepdims=True)
    ints_vec[1:2] = jnp.sum(jnp.where(diagonal, late, 0), axis=0, keepdims=True)

    second = jnp.zeros(swath.shape, jnp.int32)
    for g in range(per):
        inside = (block == me) & (group == g)
        latest = jnp.max(jnp.where(inside, index, -1), axis=1, keepdims=True)
        second = jnp.where(inside & (index == latest), 1, second)
    slot = 2 * source + second
    day, lane32 = (lax.broadcasted_iota(jnp.int32, (days, 128), k) for k in range(2))
    hit = jnp.zeros((days, 128), jnp.int32)
    for r in range(swath.shape[0]):
        hit += jnp.where(swath[r : r + 1] == days * me + day, slot[r : r + 1], 0)
    arrived = jnp.clip(jnp.sum(hit, axis=1, keepdims=True), 0, days - 1)
    ints_vec[2:3] = jnp.sum(jnp.where(day == lane32, arrived, 0), axis=0, keepdims=True)

    lag = (days - 1 - lax.broadcasted_iota(jnp.int32, (1, 128), 1)).astype(jnp.float32)
    decay = jnp.exp(lag * math.log(DECAY))
    floats_vec[0:1] = decay
    floats_vec[1:2] = lag * (1.0 / UNIT)
    floats_vec[2:3] = RIDGE * decay


def exchange_kernel(
    days, swath_ref, x_hbm, w_hbm, mask_hbm,
    slope_ref, halo_ref, mhalo_ref,
    x_ref, w_ref, mask_ref, ints_vec, floats_vec, ints_ref, floats_ref, stage, recv0, recv1, recv2, tsend, trecv, csend, crecv, edge, hrecv, mrecv,
    g_send, g_recv, t_send, t_recv, c_send, c_recv, h_send, h_recv, m_send, m_recv,
    load_sem,
):
    me = lax.axis_index("tm")
    tile = lax.axis_index("tile")
    z, y = me // 4, lax.rem(me, 4)
    peers = [lax.rem(z + dz, 4) * 4 + lax.rem(y + dy, 4) for dz, dy in OFFSETS]
    above, below = lax.rem(tile + 7, 8), lax.rem(tile + 1, 8)
    nchunk = len(CHUNKS)
    recv = (recv0, recv1, recv2)

    loads = [
        pltpu.make_async_copy(src, dst, load_sem.at[k])
        for k, (src, dst) in enumerate(((x_hbm, x_ref), (w_hbm, w_ref), (mask_hbm, mask_ref)))
    ]
    for load in loads:
        load.start()
    barrier = pltpu.get_barrier_semaphore()
    for p in peers:
        pl.semaphore_signal(barrier, inc=1, device_id={"tm": p}, device_id_type=MESH)
    for t in (above, below):
        pl.semaphore_signal(barrier, inc=1, device_id={"tile": t}, device_id_type=MESH)

    write_tables(days, me, swath_ref, ints_vec, floats_vec)
    loads += [
        pltpu.make_async_copy(ints_vec, ints_ref, load_sem.at[3]),
        pltpu.make_async_copy(floats_vec, floats_ref, load_sem.at[4]),
    ]
    for load in loads[3:]:
        load.start()
    for load in loads:
        load.wait()

    def place(k, _):
        i = ints_ref[lax.rem(k, 2), k // 2]
        for c in range(nchunk):
            stage[c, k, 0] = x_ref[i, 4 * c : 4 * c + 4]
            stage[c, k, 1] = w_ref[i, 4 * c : 4 * c + 4]
        return _

    lax.fori_loop(0, days, place, 0)
    for j in range(2):
        i = ints_ref[j, me]
        for c in range(nchunk):
            recv[c][2 * me + j, 0] = x_ref[i, 4 * c : 4 * c + 4]
            recv[c][2 * me + j, 1] = w_ref[i, 4 * c : 4 * c + 4]
    pl.semaphore_wait(barrier, len(peers) + 2)

    def remote(src, dst, send, arrive, where):
        pltpu.make_async_remote_copy(
            src_ref=src, dst_ref=dst, send_sem=send, recv_sem=arrive,
            device_id=where, device_id_type=MESH,
        ).start()

    def send_granules(c):
        for p in peers:
            remote(
                stage.at[c, pl.ds(2 * p, 2)], recv[c].at[pl.ds(2 * me, 2)],
                g_send.at[c], g_recv.at[c], {"tm": p},
            )

    def block_totals(c):
        wait_bytes(recv[c].at[pl.ds(0, 30)], g_recv.at[c])
        for g in range(4 // GROUP):
            def add(d, state):
                zeroth, first, second, level, slope = state
                a, u = floats_ref[0, d], floats_ref[1, d]
                s = ints_ref[2, d]
                v = recv[c][s, 0, GROUP * g : GROUP * (g + 1)].astype(jnp.float32)
                w = recv[c][s, 1, GROUP * g : GROUP * (g + 1)].astype(jnp.float32) * a
                wu = w * u
                p = w * v
                return (zeroth + w, first + wu, second + wu * u, level + p, slope + p * u)

            empty = jnp.zeros((GROUP, 16, 128), jnp.float32)
            state = lax.fori_loop(0, days, add, (empty,) * 5)
            for m in range(5):
                for q in range(GROUP):
                    for k in range(4):
                        tsend[c, 4 * (GROUP * g + q) + k, m] = state[m][q, 4 * k : 4 * k + 4, :]
        trecv[c, me] = tsend[c, me]
        for p in peers:
            remote(tsend.at[c, p], trecv.at[c, me], t_send.at[c], t_recv.at[c], {"tm": p})

    factor, offset = DECAY**days, days / UNIT

    def carries(c):
        wait_bytes(trecv.at[c, pl.ds(0, 15)], t_recv.at[c])
        state = [jnp.zeros((4, 128), jnp.float32)] * 5
        for b in range(16):
            zeroth, first, second, level, slope = state
            moved = (
                factor * zeroth,
                factor * (first + offset * zeroth),
                factor * (second + (2 * offset) * first + (offset * offset) * zeroth),
                factor * level,
                factor * (slope + offset * level),
            )
            for m in range(5):
                csend[c, b, m] = moved[m]
            state = [moved[m] + trecv[c, b, m] for m in range(5)]
        crecv[c, me] = csend[c, me]
        for p in peers:
            remote(csend.at[c, p], crecv.at[c, me], c_send.at[c], c_recv.at[c], {"tm": p})

    def slopes(c):
        wait_bytes(crecv.at[c, pl.ds(0, 15)], c_recv.at[c])
        for g in range(4 // GROUP):
            start = tuple(
                jnp.stack([
                    jnp.concatenate([crecv[c, 4 * (GROUP * g + q) + k, m] for k in range(4)], axis=0)
                    for q in range(GROUP)
                ])
                for m in range(5)
            )

            def advance(d, state):
                zeroth, first, second, level, slope = state
                s = ints_ref[2, d]
                a, u, ridge = (floats_ref[n, d] for n in range(3))
                v = recv[c][s, 0, GROUP * g : GROUP * (g + 1)].astype(jnp.float32)
                w = recv[c][s, 1, GROUP * g : GROUP * (g + 1)].astype(jnp.float32) * a
                wu = w * u
                p = w * v
                zeroth, first, second = zeroth + w, first + wu, second + wu * u
                level, slope = level + p, slope + p * u
                det = zeroth * (second + ridge) - first * first
                out = (first * level - zeroth * slope) / det
                for q in range(GROUP):
                    for h in range(2):
                        lanes = pl.ds(128 * (2 * (GROUP * g + q) + h), 128)
                        value = out[q, 8 * h : 8 * h + 8, :]
                        value = jnp.where(mask_ref[8 * c : 8 * c + 8, lanes] > 0, value, 0.0)
                        slope_ref[d, 8 * c : 8 * c + 8, lanes] = value
                return (zeroth, first, second, level, slope)

            lax.fori_loop(0, days, advance, start)

        def widen(d, _):
            value = lane_sum(slope_ref[d, 8 * c : 8 * c + 8])
            slope_ref[d, 8 * c : 8 * c + 8] = value
            for k in range(value.shape[1] // 128):
                if c == 0:
                    edge[0, d, k : k + 1] = value[0:1, 128 * k : 128 * k + 128]
                if c == nchunk - 1:
                    edge[1, d, k : k + 1] = value[7:8, 128 * k : 128 * k + 128]
            return _

        lax.fori_loop(0, days, widen, 0)
        if c == 0:
            remote(edge.at[0], hrecv.at[1], h_send.at[0], h_recv.at[1], {"tile": above})
        if c == nchunk - 1:
            remote(edge.at[1], hrecv.at[0], h_send.at[1], h_recv.at[0], {"tile": below})

    remote(mask_ref.at[0:8], mrecv.at[1], m_send.at[0], m_recv.at[1], {"tile": above})
    remote(mask_ref.at[16:24], mrecv.at[0], m_send.at[1], m_recv.at[0], {"tile": below})

    first, middle, last = CHUNKS
    send_granules(first)
    send_granules(middle)
    block_totals(first)
    send_granules(last)
    block_totals(middle)
    carries(first)
    block_totals(last)
    carries(middle)
    slopes(first)
    carries(last)
    slopes(middle)
    slopes(last)

    for n in range(2):
        wait_bytes(mrecv.at[n], m_recv.at[n])
        wait_bytes(hrecv.at[n], h_recv.at[n])
    for n, present in enumerate((tile > 0, tile < 7)):
        inner = jnp.where(present, 1, 0)
        halo_ref[n] = hrecv[n] * inner.astype(jnp.float32)
        mhalo_ref[n] = mrecv[n] * inner
    for c in range(nchunk):
        wait_bytes(stage.at[c, pl.ds(0, 30)], g_send.at[c])
        wait_bytes(tsend.at[c, pl.ds(0, 15)], t_send.at[c])
        wait_bytes(csend.at[c, pl.ds(0, 15)], c_send.at[c])
    for n in range(2):
        wait_bytes(edge.at[n], h_send.at[n])
        wait_bytes(mask_ref.at[0:8], m_send.at[n])


def lane_sum(field):
    width = field.shape[1]
    column = lax.broadcasted_iota(jnp.int32, field.shape, 1)
    left = jnp.where(column == 0, 0.0, pltpu.roll(field, 1, 1))
    right = jnp.where(column == width - 1, 0.0, pltpu.roll(field, width - 1, 1))
    return field + left + right


def row_sum(field, up, down):
    return (
        field
        + jnp.concatenate([up, field[:-1]], axis=0)
        + jnp.concatenate([field[1:], down], axis=0)
    )


def row_of(pieces):
    return jnp.concatenate([pieces[k : k + 1] for k in range(pieces.shape[0])], axis=1)


def smooth_kernel(per, wide_ref, halo_ref, mask_ref, mhalo_ref, out_ref, inverse, ready, sems):
    count = row_sum(
        mask_ref[...].astype(jnp.float32),
        mhalo_ref[0, 7:8].astype(jnp.float32),
        mhalo_ref[1, 0:1].astype(jnp.float32),
    )
    inverse[...] = 1.0 / jnp.maximum(lane_sum(count), 1.0)
    steps = ready.shape[0] // per

    def put(step):
        part = pl.ds(step * per, per)
        return pltpu.make_async_copy(ready.at[part], out_ref.at[part], sems.at[step])

    for step in range(steps):
        def day(n, _):
            d = step * per + n
            up = row_of(halo_ref[0, d])
            down = row_of(halo_ref[1, d])
            ready[d] = row_sum(wide_ref[d], up, down) * inverse[...]
            return _

        lax.fori_loop(0, per, day, 0)
        put(step).start()
    for step in range(steps):
        put(step).wait()


def tiled(array):
    days, rows, width = array.shape
    parts = array.reshape(days, rows // 8, 8, width // 256, 2, 128)
    return parts.transpose(0, 1, 3, 4, 2, 5).reshape(days, rows // 8 * (width // 256), 16, 128)


def on_device(ocean_heat_anomaly, observation_reliability, swath_date_number, marine_cell_flag):
    n = lax.axis_size("tm")
    days, rows, width = ocean_heat_anomaly.shape
    f32, bf16 = jnp.float32, jnp.bfloat16
    vmem = pl.BlockSpec(memory_space=pltpu.VMEM)
    hbm = pl.BlockSpec(memory_space=pltpu.HBM)
    sem = pltpu.SemaphoreType.DMA
    slope, halo, mhalo = pl.pallas_call(
        functools.partial(exchange_kernel, days),
        out_shape=(
            jax.ShapeDtypeStruct((days, rows, width), f32),
            jax.ShapeDtypeStruct((2, days, width // 128, 128), f32),
            jax.ShapeDtypeStruct((2, 8, width), jnp.int32),
        ),
        in_specs=[vmem, hbm, hbm, hbm],
        out_specs=(vmem, vmem, vmem),
        scratch_shapes=[
            pltpu.VMEM((days, rows // 8 * (width // 256), 16, 128), bf16),
            pltpu.VMEM((days, rows // 8 * (width // 256), 16, 128), bf16),
            pltpu.VMEM((rows, width), jnp.int32),
            pltpu.VMEM((8, 128), jnp.int32),
            pltpu.VMEM((8, 128), f32),
            pltpu.SMEM((8, 128), jnp.int32),
            pltpu.SMEM((8, 128), f32),
            pltpu.VMEM((3, days, 2, 4, 16, 128), bf16),
            pltpu.VMEM((days, 2, 4, 16, 128), bf16),
            pltpu.VMEM((days, 2, 4, 16, 128), bf16),
            pltpu.VMEM((days, 2, 4, 16, 128), bf16),
            pltpu.VMEM((3, n, 5, 4, 128), f32),
            pltpu.VMEM((3, n, 5, 4, 128), f32),
            pltpu.VMEM((3, n, 5, 4, 128), f32),
            pltpu.VMEM((3, n, 5, 4, 128), f32),
            pltpu.VMEM((2, days, width // 128, 128), f32),
            pltpu.VMEM((2, days, width // 128, 128), f32),
            pltpu.VMEM((2, 8, width), jnp.int32),
        ] + [sem((3,))] * 6 + [sem((2,))] * 4 + [sem((5,))],
        compiler_params=pltpu.CompilerParams(
            collective_id=0, has_side_effects=True, vmem_limit_bytes=24 << 20
        ),
    )(
        swath_date_number.reshape(4, 128),
        pltpu.with_memory_space_constraint(tiled(ocean_heat_anomaly), pltpu.HBM),
        pltpu.with_memory_space_constraint(tiled(observation_reliability), pltpu.HBM),
        pltpu.with_memory_space_constraint(marine_cell_flag, pltpu.HBM),
    )
    per = 4
    return pl.pallas_call(
        functools.partial(smooth_kernel, per),
        out_shape=jax.ShapeDtypeStruct((days, rows, width), f32),
        in_specs=[vmem] * 4,
        out_specs=pl.BlockSpec(memory_space=pl.ANY),
        scratch_shapes=[
            pltpu.VMEM((rows, width), f32),
            pltpu.VMEM((days, rows, width), f32),
            sem((days // per,)),
        ],
        compiler_params=pltpu.CompilerParams(vmem_limit_bytes=16 << 20),
    )(slope, halo, marine_cell_flag, mhalo)


def solution(mesh):
    in_specs = (P("tm", "tile", None), P("tm", "tile", None), P(), P("tile", None))
    out_specs = P("tm", "tile", None)
    return jax.shard_map(
        on_device, mesh=mesh, in_specs=in_specs, out_specs=out_specs, check_vma=False
    )
```

time: 76.1 us -> 66.7 us (0.88)
  Pallas kernels: 71.5 us -> 65.7 us
  other arithmetic: 2.86 us -> 0 us
    pallas_call x1, Pallas kernels: 7.29 us -> 1.97 us  [on_device(): pl.pallas_call(functools.partial(smooth_kernel, per), out_shape=jax.Shape...]
    reduce_sum x5 -> x0, other arithmetic: 1.44 us -> none  [the longest x1 0.68 us: tables(): slot_of_day = jnp.sum(jnp.where(hit, slot[None], 0), axis=(1, 2))]
where the time goes in v2:
time: 66.7 us; the launch traced here: 66.5 us
  Pallas kernels  65.7 us (99%)
  local copies, waits for them, and re-layouts  0.72 us (1%)
    pallas_call x1, Pallas kernels, on_device(): pl.pallas_call(functools.partial(exchange_kernel, days), out_shape=(jax.S...  63.8 us
    pallas_call x1, Pallas kernels, on_device(): pl.pallas_call(functools.partial(smooth_kernel, per), out_shape=jax.Shape...  1.97 us

profile of v2, /device:TPU:2, one launch (start us, length us, event | category | flops | bytes accessed | tf_op | source)
XLA Modules:
  0.0 66.5 jit_solution(7823351223540695614)
XLA Ops:
  0.0 0.0 copy-start
  0.0 0.0 copy-start.1
  0.0 0.7 %copy-done.1 = s32[512]{0:T(512)S(1)} copy-done((s32[512]{0:T(512)S(1)}, s32[512]{0:T(512)}, u32[]{:S(2)}) %copy-start.1) | copy-done | bytes 2072
  0.7 63.8 %shard_map.46 = (f32[32,24,1024]{2,1,0:T(8,128)S(1)}, f32[2,32,8,128]{3,2,1,0:T(8,128)S(1)}, s32[2,8,1024]{2,1,0:T(8,128)S(1)}) custom-call(s32[4,128]{1,0:T(4,128)S(1)} %bitcast.11, bf16[32,12,16,128]{3,2,1,0:T(8,128)(2,1)} %bitcast.12, bf16[32,12,16,128]{3,2,1,0:T(8,128)(2,1)} %bitcast.13, s32[24,1024]{1,0:T(8,128)} %mask_ref.1), custom_call_target="tpu_custom_call" | custom-call | tf_op jit(solution)/shard_map/pallas_call | solution.py:316
  64.5 0.0 copy-done
  64.5 2.0 %shard_map.47 = f32[32,24,1024]{2,1,0:T(8,128)} custom-call(f32[32,24,1024]{2,1,0:T(8,128)S(1)} %get-tuple-element.8.wide_ref, f32[2,32,8,128]{3,2,1,0:T(8,128)S(1)} %get-tuple-element.9.halo_ref, s32[24,1024]{1,0:T(8,128)S(1)} %copy-done, s32[2,8,1024]{2,1,0:T(8,128)S(1)} %get-tuple-element.10.mhalo_ref), custom_call_target="tpu_custom_call" | custom-call | tf_op jit(solution)/shard_map/pallas_call | solution.py:355
Async XLA Ops:
  0.0 64.5 %copy-start = (s32[24,1024]{1,0:T(8,128)S(1)}, s32[24,1024]{1,0:T(8,128)}, u32[]{:S(2)}) copy-start(s32[24,1024]{1,0:T(8,128)} %mask_ref.1) | copy-start | bytes 294916
  0.0 0.7 %copy-start.1 = (s32[512]{0:T(512)S(1)}, s32[512]{0:T(512)}, u32[]{:S(2)}) copy-start(s32[512]{0:T(512)} %param.6) | copy-start | bytes 6148

commit v3 on v2

--- a/solution.py
+++ b/solution.py
@@ -19,6 +19,16 @@
 )
 CHUNKS = (0, 2, 1)
 GROUP = 2
+UNROLL_ADD, UNROLL_ADVANCE, UNROLL_WIDEN, UNROLL_PLACE = 4, 4, 4, 4
+
+
+def repeat(count, body, start, unroll):
+    def several(k, state):
+        for n in range(unroll):
+            state = body(k * unroll + n, state)
+        return state
+
+    return lax.fori_loop(0, count // unroll, several, start)
 
 
 def wait_bytes(ref, sem):
@@ -63,9 +73,9 @@
 
 
 def exchange_kernel(
-    days, swath_ref, x_hbm, w_hbm, mask_hbm,
+    days, swath_hbm, x_hbm, w_hbm, mask_hbm,
     slope_ref, halo_ref, mhalo_ref,
-    x_ref, w_ref, mask_ref, ints_vec, floats_vec, ints_ref, floats_ref, stage, recv0, recv1, recv2, tsend, trecv, csend, crecv, edge, hrecv, mrecv,
+    swath_ref, x_ref, w_ref, mask_ref, ints_vec, floats_vec, ints_ref, floats_ref, stage, recv0, recv1, recv2, tsend, trecv, csend, crecv, edge, hrecv, mrecv,
     g_send, g_recv, t_send, t_recv, c_send, c_recv, h_send, h_recv, m_send, m_recv,
     load_sem,
 ):
@@ -77,9 +87,9 @@
     nchunk = len(CHUNKS)
     recv = (recv0, recv1, recv2)
 
+    pairs = ((swath_hbm, swath_ref), (x_hbm, x_ref), (w_hbm, w_ref), (mask_hbm, mask_ref))
     loads = [
-        pltpu.make_async_copy(src, dst, load_sem.at[k])
-        for k, (src, dst) in enumerate(((x_hbm, x_ref), (w_hbm, w_ref), (mask_hbm, mask_ref)))
+        pltpu.make_async_copy(src, dst, load_sem.at[k]) for k, (src, dst) in enumerate(pairs)
     ]
     for load in loads:
         load.start()
@@ -89,29 +99,31 @@
     for t in (above, below):
         pl.semaphore_signal(barrier, inc=1, device_id={"tile": t}, device_id_type=MESH)
 
+    loads[0].wait()
     write_tables(days, me, swath_ref, ints_vec, floats_vec)
     loads += [
-        pltpu.make_async_copy(ints_vec, ints_ref, load_sem.at[3]),
-        pltpu.make_async_copy(floats_vec, floats_ref, load_sem.at[4]),
+        pltpu.make_async_copy(ints_vec, ints_ref, load_sem.at[4]),
+        pltpu.make_async_copy(floats_vec, floats_ref, load_sem.at[5]),
     ]
-    for load in loads[3:]:
+    for load in loads[4:]:
         load.start()
-    for load in loads:
+    for load in loads[1:]:
         load.wait()
 
-    def place(k, _):
-        i = ints_ref[lax.rem(k, 2), k // 2]
-        for c in range(nchunk):
+    def stage_chunk(c):
+        def place(k, _):
+            i = ints_ref[lax.rem(k, 2), k // 2]
             stage[c, k, 0] = x_ref[i, 4 * c : 4 * c + 4]
             stage[c, k, 1] = w_ref[i, 4 * c : 4 * c + 4]
-        return _
-
-    lax.fori_loop(0, days, place, 0)
-    for j in range(2):
-        i = ints_ref[j, me]
-        for c in range(nchunk):
+            return _
+
+        repeat(days, place, 0, UNROLL_PLACE)
+        for j in range(2):
+            i = ints_ref[j, me]
             recv[c][2 * me + j, 0] = x_ref[i, 4 * c : 4 * c + 4]
             recv[c][2 * me + j, 1] = w_ref[i, 4 * c : 4 * c + 4]
+
+    stage_chunk(CHUNKS[0])
     pl.semaphore_wait(barrier, len(peers) + 2)
 
     def remote(src, dst, send, arrive, where):
@@ -141,7 +153,7 @@
                 return (zeroth + w, first + wu, second + wu * u, level + p, slope + p * u)
 
             empty = jnp.zeros((GROUP, 16, 128), jnp.float32)
-            state = lax.fori_loop(0, days, add, (empty,) * 5)
+            state = repeat(days, add, (empty,) * 5, UNROLL_ADD)
             for m in range(5):
                 for q in range(GROUP):
                     for k in range(4):
@@ -202,7 +214,7 @@
                         slope_ref[d, 8 * c : 8 * c + 8, lanes] = value
                 return (zeroth, first, second, level, slope)
 
-            lax.fori_loop(0, days, advance, start)
+            repeat(days, advance, start, UNROLL_ADVANCE)
 
         def widen(d, _):
             value = lane_sum(slope_ref[d, 8 * c : 8 * c + 8])
@@ -214,7 +226,7 @@
                     edge[1, d, k : k + 1] = value[7:8, 128 * k : 128 * k + 128]
             return _
 
-        lax.fori_loop(0, days, widen, 0)
+        repeat(days, widen, 0, UNROLL_WIDEN)
         if c == 0:
             remote(edge.at[0], hrecv.at[1], h_send.at[0], h_recv.at[1], {"tile": above})
         if c == nchunk - 1:
@@ -225,7 +237,9 @@
 
     first, middle, last = CHUNKS
     send_granules(first)
+    stage_chunk(middle)
     send_granules(middle)
+    stage_chunk(last)
     block_totals(first)
     send_granules(last)
     block_totals(middle)
@@ -294,7 +308,7 @@
             ready[d] = row_sum(wide_ref[d], up, down) * inverse[...]
             return _
 
-        lax.fori_loop(0, per, day, 0)
+        repeat(per, day, 0, per)
         put(step).start()
     for step in range(steps):
         put(step).wait()
@@ -320,9 +334,10 @@
             jax.ShapeDtypeStruct((2, days, width // 128, 128), f32),
             jax.ShapeDtypeStruct((2, 8, width), jnp.int32),
         ),
-        in_specs=[vmem, hbm, hbm, hbm],
+        in_specs=[hbm] * 4,
         out_specs=(vmem, vmem, vmem),
         scratch_shapes=[
+            pltpu.VMEM((4, 128), jnp.int32),
             pltpu.VMEM((days, rows // 8 * (width // 256), 16, 128), bf16),
             pltpu.VMEM((days, rows // 8 * (width // 256), 16, 128), bf16),
             pltpu.VMEM((rows, width), jnp.int32),
@@ -341,12 +356,12 @@
             pltpu.VMEM((2, days, width // 128, 128), f32),
             pltpu.VMEM((2, days, width // 128, 128), f32),
             pltpu.VMEM((2, 8, width), jnp.int32),
-        ] + [sem((3,))] * 6 + [sem((2,))] * 4 + [sem((5,))],
+        ] + [sem((3,))] * 6 + [sem((2,))] * 4 + [sem((6,))],
         compiler_params=pltpu.CompilerParams(
             collective_id=0, has_side_effects=True, vmem_limit_bytes=24 << 20
         ),
     )(
-        swath_date_number.reshape(4, 128),
+        pltpu.with_memory_space_constraint(swath_date_number.reshape(4, 128), pltpu.HBM),
         pltpu.with_memory_space_constraint(tiled(ocean_heat_anomaly), pltpu.HBM),
         pltpu.with_memory_space_constraint(tiled(observation_reliability), pltpu.HBM),
         pltpu.with_memory_space_constraint(marine_cell_flag, pltpu.HBM),

time: 66.7 us -> 62.6 us (0.939)
  Pallas kernels: 65.7 us -> 62.3 us
  local copies, waits for them, and re-layouts: 0.72 us -> 0.01 us
    pallas_call x1, Pallas kernels: 63.8 us -> 60.4 us  [on_device(): pl.pallas_call(functools.partial(exchange_kernel, days), out_shape=(jax.S...]
    unnamed x4 -> x2, local copies, waits for them, and re-layouts: 0.72 us -> 0.01 us
where the time goes in v3:
time: 62.6 us; the launch traced here: 62.3 us
  Pallas kernels  62.3 us (100%)
    pallas_call x1, Pallas kernels, on_device(): pl.pallas_call(functools.partial(exchange_kernel, days), out_shape=(jax.S...  60.4 us
    pallas_call x1, Pallas kernels, on_device(): pl.pallas_call(functools.partial(smooth_kernel, per), out_shape=jax.Shape...  1.89 us

profile of v3, /device:TPU:2, one launch (start us, length us, event | category | flops | bytes accessed | tf_op | source)
XLA Modules:
  0.0 62.3 jit_solution(11520848292486584342)
XLA Ops:
  0.0 0.0 copy-start
  0.0 60.4 %shard_map.46 = (f32[32,24,1024]{2,1,0:T(8,128)S(1)}, f32[2,32,8,128]{3,2,1,0:T(8,128)S(1)}, s32[2,8,1024]{2,1,0:T(8,128)S(1)}) custom-call(s32[4,128]{1,0:T(4,128)} %bitcast.13, bf16[32,12,16,128]{3,2,1,0:T(8,128)(2,1)} %bitcast.11, bf16[32,12,16,128]{3,2,1,0:T(8,128)(2,1)} %bitcast.12, s32[24,1024]{1,0:T(8,128)} %mask_ref.1), custom_call_target="tpu_custom_call" | custom-call | tf_op jit(solution)/shard_map/pallas_call | solution.py:330
  60.4 0.0 copy-done
  60.4 1.9 %shard_map.47 = f32[32,24,1024]{2,1,0:T(8,128)} custom-call(f32[32,24,1024]{2,1,0:T(8,128)S(1)} %get-tuple-element.8.wide_ref, f32[2,32,8,128]{3,2,1,0:T(8,128)S(1)} %get-tuple-element.9.halo_ref, s32[24,1024]{1,0:T(8,128)S(1)} %copy-done, s32[2,8,1024]{2,1,0:T(8,128)S(1)} %get-tuple-element.10.mhalo_ref), custom_call_target="tpu_custom_call" | custom-call | tf_op jit(solution)/shard_map/pallas_call | solution.py:370
Async XLA Ops:
  0.0 60.4 %copy-start = (s32[24,1024]{1,0:T(8,128)S(1)}, s32[24,1024]{1,0:T(8,128)}, u32[]{:S(2)}) copy-start(s32[24,1024]{1,0:T(8,128)} %mask_ref.1) | copy-start | bytes 294916

commit v4 on v3

--- a/solution.py
+++ b/solution.py
@@ -14,8 +14,8 @@
 MESH = pl.DeviceIdType.MESH
 
 OFFSETS = (
-    (0, 1), (1, 0), (0, 3), (3, 0), (1, 1), (3, 3), (1, 3), (3, 1),
-    (2, 0), (0, 2), (2, 1), (1, 2), (2, 3), (3, 2), (2, 2),
+    (2, 2), (2, 1), (1, 2), (2, 3), (3, 2), (2, 0), (0, 2), (1, 1),
+    (3, 3), (1, 3), (3, 1), (0, 1), (1, 0), (0, 3), (3, 0),
 )
 CHUNKS = (0, 2, 1)
 GROUP = 2

time: 62.6 us -> 61 us (0.974)
  Pallas kernels: 62.3 us -> 60.7 us
    pallas_call x1, Pallas kernels: 60.4 us -> 58.9 us  [on_device(): pl.pallas_call(functools.partial(exchange_kernel, days), out_shape=(jax.S...]
where the time goes in v4:
time: 61 us; the launch traced here: 60.8 us
  Pallas kernels  60.7 us (100%)
    pallas_call x1, Pallas kernels, on_device(): pl.pallas_call(functools.partial(exchange_kernel, days), out_shape=(jax.S...  58.9 us
    pallas_call x1, Pallas kernels, on_device(): pl.pallas_call(functools.partial(smooth_kernel, per), out_shape=jax.Shape...  1.89 us

profile of v4, /device:TPU:2, one launch (start us, length us, event | category | flops | bytes accessed | tf_op | source)
XLA Modules:
  0.0 60.8 jit_solution(7965190868716874145)
XLA Ops:
  0.0 0.0 copy-start
  0.0 58.9 %shard_map.46 = (f32[32,24,1024]{2,1,0:T(8,128)S(1)}, f32[2,32,8,128]{3,2,1,0:T(8,128)S(1)}, s32[2,8,1024]{2,1,0:T(8,128)S(1)}) custom-call(s32[4,128]{1,0:T(4,128)} %bitcast.13, bf16[32,12,16,128]{3,2,1,0:T(8,128)(2,1)} %bitcast.11, bf16[32,12,16,128]{3,2,1,0:T(8,128)(2,1)} %bitcast.12, s32[24,1024]{1,0:T(8,128)} %mask_ref.1), custom_call_target="tpu_custom_call" | custom-call | tf_op jit(solution)/shard_map/pallas_call | solution.py:330
  58.9 0.0 copy-done
  58.9 1.9 %shard_map.47 = f32[32,24,1024]{2,1,0:T(8,128)} custom-call(f32[32,24,1024]{2,1,0:T(8,128)S(1)} %get-tuple-element.8.wide_ref, f32[2,32,8,128]{3,2,1,0:T(8,128)S(1)} %get-tuple-element.9.halo_ref, s32[24,1024]{1,0:T(8,128)S(1)} %copy-done, s32[2,8,1024]{2,1,0:T(8,128)S(1)} %get-tuple-element.10.mhalo_ref), custom_call_target="tpu_custom_call" | custom-call | tf_op jit(solution)/shard_map/pallas_call | solution.py:370
Async XLA Ops:
  0.0 58.9 %copy-start = (s32[24,1024]{1,0:T(8,128)S(1)}, s32[24,1024]{1,0:T(8,128)}, u32[]{:S(2)}) copy-start(s32[24,1024]{1,0:T(8,128)} %mask_ref.1) | copy-start | bytes 294916

commit v5 on v4

--- a/solution.py
+++ b/solution.py
@@ -19,7 +19,7 @@
 )
 CHUNKS = (0, 2, 1)
 GROUP = 2
-UNROLL_ADD, UNROLL_ADVANCE, UNROLL_WIDEN, UNROLL_PLACE = 4, 4, 4, 4
+UNROLL_ADD, UNROLL_ADVANCE, UNROLL_WIDEN, UNROLL_PLACE = 8, 8, 8, 4
 
 
 def repeat(count, body, start, unroll):

time: 61 us -> 60.3 us (0.989)
  Pallas kernels: 60.7 us -> 60 us
    pallas_call x1, Pallas kernels: 58.9 us -> 58.1 us  [on_device(): pl.pallas_call(functools.partial(exchange_kernel, days), out_shape=(jax.S...]
where the time goes in v5:
time: 60.3 us; the launch traced here: 60 us
  Pallas kernels  60 us (100%)
    pallas_call x1, Pallas kernels, on_device(): pl.pallas_call(functools.partial(exchange_kernel, days), out_shape=(jax.S...  58.1 us
    pallas_call x1, Pallas kernels, on_device(): pl.pallas_call(functools.partial(smooth_kernel, per), out_shape=jax.Shape...  1.89 us

profile of v5, /device:TPU:2, one launch (start us, length us, event | category | flops | bytes accessed | tf_op | source)
XLA Modules:
  0.0 60.0 jit_solution(3675143570358223051)
XLA Ops:
  0.0 0.0 copy-start
  0.0 58.1 %shard_map.46 = (f32[32,24,1024]{2,1,0:T(8,128)S(1)}, f32[2,32,8,128]{3,2,1,0:T(8,128)S(1)}, s32[2,8,1024]{2,1,0:T(8,128)S(1)}) custom-call(s32[4,128]{1,0:T(4,128)} %bitcast.13, bf16[32,12,16,128]{3,2,1,0:T(8,128)(2,1)} %bitcast.11, bf16[32,12,16,128]{3,2,1,0:T(8,128)(2,1)} %bitcast.12, s32[24,1024]{1,0:T(8,128)} %mask_ref.1), custom_call_target="tpu_custom_call" | custom-call | tf_op jit(solution)/shard_map/pallas_call | solution.py:330
  58.1 0.0 copy-done
  58.1 1.9 %shard_map.47 = f32[32,24,1024]{2,1,0:T(8,128)} custom-call(f32[32,24,1024]{2,1,0:T(8,128)S(1)} %get-tuple-element.8.wide_ref, f32[2,32,8,128]{3,2,1,0:T(8,128)S(1)} %get-tuple-element.9.halo_ref, s32[24,1024]{1,0:T(8,128)S(1)} %copy-done, s32[2,8,1024]{2,1,0:T(8,128)S(1)} %get-tuple-element.10.mhalo_ref), custom_call_target="tpu_custom_call" | custom-call | tf_op jit(solution)/shard_map/pallas_call | solution.py:370
Async XLA Ops:
  0.0 58.1 %copy-start = (s32[24,1024]{1,0:T(8,128)S(1)}, s32[24,1024]{1,0:T(8,128)}, u32[]{:S(2)}) copy-start(s32[24,1024]{1,0:T(8,128)} %mask_ref.1) | copy-start | bytes 294916

commit v6 on v5

--- a/solution.py
+++ b/solution.py
@@ -19,7 +19,7 @@
 )
 CHUNKS = (0, 2, 1)
 GROUP = 2
-UNROLL_ADD, UNROLL_ADVANCE, UNROLL_WIDEN, UNROLL_PLACE = 8, 8, 8, 4
+UNROLL_ADD, UNROLL_ADVANCE, UNROLL_WIDEN, UNROLL_PLACE = 16, 16, 16, 8
 
 
 def repeat(count, body, start, unroll):

time: 60.3 us -> 60 us (level)
  no operation moved by 1% of the time
where the time goes in v6:
time: 60 us; the launch traced here: 59.8 us
  Pallas kernels  59.8 us (100%)
    pallas_call x1, Pallas kernels, on_device(): pl.pallas_call(functools.partial(exchange_kernel, days), out_shape=(jax.S...  57.9 us
    pallas_call x1, Pallas kernels, on_device(): pl.pallas_call(functools.partial(smooth_kernel, per), out_shape=jax.Shape...  1.89 us

profile of v6, /device:TPU:2, one launch (start us, length us, event | category | flops | bytes accessed | tf_op | source)
XLA Modules:
  0.0 59.8 jit_solution(13202496052510342240)
XLA Ops:
  0.0 0.0 copy-start
  0.0 57.9 %shard_map.46 = (f32[32,24,1024]{2,1,0:T(8,128)S(1)}, f32[2,32,8,128]{3,2,1,0:T(8,128)S(1)}, s32[2,8,1024]{2,1,0:T(8,128)S(1)}) custom-call(s32[4,128]{1,0:T(4,128)} %bitcast.13, bf16[32,12,16,128]{3,2,1,0:T(8,128)(2,1)} %bitcast.11, bf16[32,12,16,128]{3,2,1,0:T(8,128)(2,1)} %bitcast.12, s32[24,1024]{1,0:T(8,128)} %mask_ref.1), custom_call_target="tpu_custom_call" | custom-call | tf_op jit(solution)/shard_map/pallas_call | solution.py:330
  57.9 0.0 copy-done
  57.9 1.9 %shard_map.47 = f32[32,24,1024]{2,1,0:T(8,128)} custom-call(f32[32,24,1024]{2,1,0:T(8,128)S(1)} %get-tuple-element.8.wide_ref, f32[2,32,8,128]{3,2,1,0:T(8,128)S(1)} %get-tuple-element.9.halo_ref, s32[24,1024]{1,0:T(8,128)S(1)} %copy-done, s32[2,8,1024]{2,1,0:T(8,128)S(1)} %get-tuple-element.10.mhalo_ref), custom_call_target="tpu_custom_call" | custom-call | tf_op jit(solution)/shard_map/pallas_call | solution.py:370
Async XLA Ops:
  0.0 57.9 %copy-start = (s32[24,1024]{1,0:T(8,128)S(1)}, s32[24,1024]{1,0:T(8,128)}, u32[]{:S(2)}) copy-start(s32[24,1024]{1,0:T(8,128)} %mask_ref.1) | copy-start | bytes 294916

commit v7 on v6

--- a/solution.py
+++ b/solution.py
@@ -132,8 +132,8 @@
             device_id=where, device_id_type=MESH,
         ).start()
 
-    def send_granules(c):
-        for p in peers:
+    def send_granules(c, targets=peers):
+        for p in targets:
             remote(
                 stage.at[c, pl.ds(2 * p, 2)], recv[c].at[pl.ds(2 * me, 2)],
                 g_send.at[c], g_recv.at[c], {"tm": p},
@@ -238,9 +238,10 @@
     first, middle, last = CHUNKS
     send_granules(first)
     stage_chunk(middle)
-    send_granules(middle)
+    send_granules(middle, peers[:11])
     stage_chunk(last)
     block_totals(first)
+    send_granules(middle, peers[11:])
     send_granules(last)
     block_totals(middle)
     carries(first)

time: 60 us -> 60.1 us (level)
  no operation moved by 1% of the time
where the time goes in v7:
time: 60.1 us; the launch traced here: 59.9 us
  Pallas kernels  59.9 us (100%)
    pallas_call x1, Pallas kernels, on_device(): pl.pallas_call(functools.partial(exchange_kernel, days), out_shape=(jax.S...  58 us
    pallas_call x1, Pallas kernels, on_device(): pl.pallas_call(functools.partial(smooth_kernel, per), out_shape=jax.Shape...  1.89 us

profile of v7, /device:TPU:2, one launch (start us, length us, event | category | flops | bytes accessed | tf_op | source)
XLA Modules:
  0.0 59.9 jit_solution(8192043767788956668)
XLA Ops:
  0.0 0.0 copy-start
  0.0 58.0 %shard_map.46 = (f32[32,24,1024]{2,1,0:T(8,128)S(1)}, f32[2,32,8,128]{3,2,1,0:T(8,128)S(1)}, s32[2,8,1024]{2,1,0:T(8,128)S(1)}) custom-call(s32[4,128]{1,0:T(4,128)} %bitcast.13, bf16[32,12,16,128]{3,2,1,0:T(8,128)(2,1)} %bitcast.11, bf16[32,12,16,128]{3,2,1,0:T(8,128)(2,1)} %bitcast.12, s32[24,1024]{1,0:T(8,128)} %mask_ref.1), custom_call_target="tpu_custom_call" | custom-call | tf_op jit(solution)/shard_map/pallas_call | solution.py:331
  58.0 0.0 copy-done
  58.0 1.9 %shard_map.47 = f32[32,24,1024]{2,1,0:T(8,128)} custom-call(f32[32,24,1024]{2,1,0:T(8,128)S(1)} %get-tuple-element.8.wide_ref, f32[2,32,8,128]{3,2,1,0:T(8,128)S(1)} %get-tuple-element.9.halo_ref, s32[24,1024]{1,0:T(8,128)S(1)} %copy-done, s32[2,8,1024]{2,1,0:T(8,128)S(1)} %get-tuple-element.10.mhalo_ref), custom_call_target="tpu_custom_call" | custom-call | tf_op jit(solution)/shard_map/pallas_call | solution.py:371
Async XLA Ops:
  0.0 58.0 %copy-start = (s32[24,1024]{1,0:T(8,128)S(1)}, s32[24,1024]{1,0:T(8,128)}, u32[]{:S(2)}) copy-start(s32[24,1024]{1,0:T(8,128)} %mask_ref.1) | copy-start | bytes 294916
